TPU v7x, 32 devices: a 4x4x1 block of a 4x4x8 slice. The times are simulated.
32 devices in a mesh: rep: 1 (over z), fsdp: 4 (over y), ep: 8 (over x, core).
Axes of the slice: x: 4, y: 4, z: 1, core: 2. Of those that a mesh axis runs over, the one named last changes fastest.
The devices are a block of a 4x4x8 slice.
Arguments:
- tokens: bfloat16 [16384, 1536], P(('rep', 'ep', 'fsdp'))
- expert_idx: int32 [16384, 8], P(('rep', 'ep', 'fsdp'))
- gates: float32 [16384, 8], P(('rep', 'ep', 'fsdp'))
- w_gate: bfloat16 [40, 1536, 512], P('ep', 'fsdp')
- w_up: bfloat16 [40, 1536, 512], P('ep', 'fsdp')
- w_down: bfloat16 [40, 512, 1536], P('ep', None, 'fsdp')
Outputs:
- output: bfloat16 [16384, 1536], P(('rep', 'ep', 'fsdp'))
All inputs are finite; a program needn't handle non-finite values.
Results may differ from a plain program's by a relative error of at most 0.001.
Values are sent between devices in bfloat16 or wider.
A program may use at most 768 MiB of HBM per device.

v0:
```python
import jax
import jax.numpy as jnp
from jax import lax
from jax.sharding import PartitionSpec as P


def routing_matrix(expert_idx, num_experts, capacity):
    tok_count, top_k = expert_idx.shape
    flat_ids = expert_idx.reshape(tok_count * top_k)
    onehot = (flat_ids[:, None] == jnp.arange(num_experts)[None, :]).astype(jnp.int32)
    before = jnp.cumsum(onehot, axis=0) - onehot
    slot_ids = jnp.sum(before * onehot, axis=1)
    target = jnp.where(slot_ids < capacity, flat_ids * capacity + slot_ids, -1)
    select = target[:, None] == jnp.arange(num_experts * capacity)[None, :]
    return select.astype(jnp.bfloat16).reshape(tok_count, top_k, num_experts * capacity)


def solution(mesh):
    ep_size = mesh.shape['ep']
    row_spec = P(('rep', 'ep', 'fsdp'), None)

    def device_step(tokens, expert_idx, gates, w_gate, w_up, w_down):
        tok_count, top_k = expert_idx.shape
        n_local = w_gate.shape[0]
        num_experts = n_local * ep_size
        model_dim = tokens.shape[1]
        capacity = (2 * tok_count * top_k + num_experts - 1) // num_experts
        select = routing_matrix(expert_idx, num_experts, capacity)
        send_buf = jnp.einsum('tkf,td->fd', select, tokens, preferred_element_type=jnp.float32).astype(jnp.bfloat16)
        send_buf = send_buf.reshape(ep_size, n_local, capacity, model_dim)
        recv_buf = lax.all_to_all(send_buf, 'ep', 0, 0, tiled=True)
        wg_full = lax.all_gather(w_gate, 'fsdp', axis=1, tiled=True)
        wu_full = lax.all_gather(w_up, 'fsdp', axis=1, tiled=True)
        wd_full = lax.all_gather(w_down, 'fsdp', axis=2, tiled=True)
        act_a = jnp.einsum('sncd,ndf->sncf', recv_buf, wg_full, preferred_element_type=jnp.float32)
        act_b = jnp.einsum('sncd,ndf->sncf', recv_buf, wu_full, preferred_element_type=jnp.float32)
        hidden = (jax.nn.silu(act_a) * act_b).astype(jnp.bfloat16)
        expert_out = jnp.einsum('sncf,nfd->sncd', hidden, wd_full, preferred_element_type=jnp.float32).astype(jnp.bfloat16)
        back_buf = lax.all_to_all(expert_out, 'ep', 0, 0, tiled=True)
        back_rows = back_buf.reshape(num_experts * capacity, model_dim)
        pair_out = jnp.einsum('tkf,fd->tkd', select, back_rows, preferred_element_type=jnp.float32)
        mixed = tokens.astype(jnp.float32) + jnp.sum(gates[:, :, None] * pair_out, axis=1)
        return mixed.astype(jnp.bfloat16)

    return jax.shard_map(device_step, mesh=mesh, in_specs=(row_spec, row_spec, row_spec, P('ep', 'fsdp', None), P('ep', 'fsdp', None), P('ep', None, 'fsdp')), out_specs=row_spec, check_vma=False)
```

profile of v0, /device:TPU:97, one launch (start us, length us, event | category | flops | bytes accessed | tf_op | source)
XLA Modules:
  0.0 947.1 jit_solution(17018318223030928138)
XLA Ops:
  6.5 0.0 copy-start
  6.5 0.0 all-gather.6.cloned.1.call-start
  6.6 0.7 all-gather.6.cloned.1.call-update
  7.3 0.8 copy.28
  8.2 0.1 eq.65
  8.3 0.1 eq.61
  8.5 0.1 fusion.23
  8.5 11.5 %reduce-window.6 = s32[40,32,128]{2,1,0:T(8,128)S(1)} reduce-window(s32[40,32,128]{2,1,0:T(8,128)S(1)} %fusion.23, s32[]{:T(128)} %constant.4.clone.1), window={size=1x1x128 pad=0_0x0_0x127_0}, to_apply=%region_0.0 | reduce-window | flops 20807680 | bytes 1310724 | tf_op jit(solution)/shard_map/reduce-window
  20.1 0.2 slice.8
  20.3 0.3 copy.42
  20.6 0.2 reduce-window.9
  20.8 0.2 broadcast_add_fusion
  21.1 0.5 fusion.22
  21.5 0.2 reduce_sum.30
  21.7 0.7 broadcast_multiply_fusion
  22.4 0.1 copy.33
  22.6 0.1 copy.34
  22.7 0.0 copy-start.2
  22.7 65.8 %convert_reduce_fusion = bf16[512,8200]{0,1:T(8,128)(2,1)} fusion(s32[512,8]{0,1:T(8,128)S(1)} %copy.34), kind=kLoop, calls=%fused_computation | loop fusion | flops 130150400 | bytes 8413184 | tf_op jit(solution)/shard_map/tkf,td->fd/reduce_sum | solution.py:29
  88.5 0.0 copy-done
  88.6 20.4 %fusion.25 = bf16[8200,1536]{1,0:T(8,128)(2,1)} fusion(bf16[512,8200]{0,1:T(8,128)(2,1)} %convert_reduce_fusion, bf16[512,1536]{1,0:T(8,128)(2,1)S(1)} %copy-done), kind=kOutput, calls=%fused_computation.37 | convolution fusion | flops 12897484800 | bytes 35160064 | tf_op jit(solution)/shard_map/tkf,td->fd/dot_general | solution.py:29
  109.0 0.0 copy-done.2
  109.0 30.9 %reshape.67 = bf16[8,5,205,1536]{3,2,1,0:T(8,128)(2,1)} reshape(bf16[8200,1536]{1,0:T(8,128)(2,1)} %fusion.25) | data formatting | bytes 50380800 | tf_op jit(solution)/shard_map/reshape | solution.py:30
  139.9 8.5 all-to-all-start
  148.4 0.0 all-gather.4.cloned.1.call-start
  148.4 0.8 all-gather.4.cloned.1.call-update
  149.2 0.1 all-gather.8.cloned.1.call-start
  149.3 0.7 all-gather.8.cloned.1.call-update
  150.0 0.0 all-gather.6.cloned.1.call-done
  150.0 276.0 %all-to-all-done = bf16[8,5,205,1536]{3,2,1,0:T(8,128)(2,1)} async-done(((bf16[8,5,205,1536]{3,2,1,0:T(8,128)(2,1)}), bf16[8,5,205,1536]{3,2,1,0:T(8,128)(2,1)}, u32[]{:S(2)}, u32[]{:S(2)}) %all-to-all-start) | async-done | bytes 25190432 | tf_op jit(solution)/shard_map/all_to_all | solution.py:31
  426.0 23.1 %fusion.7 = f32[5,8,205,512]{3,2,1,0:T(8,128)} fusion(bf16[8,5,205,1536]{3,2,1,0:T(8,128)(2,1)} %all-to-all-done, bf16[5,1536,512]{2,1,0:T(8,128)(2,1)} %all-gather.6.cloned.1.call-done), kind=kOutput, calls=%fused_computation.10 | convolution fusion | flops 12897484800 | bytes 49848320 | tf_op jit(solution)/shard_map/sncd,ndf->sncf/dot_general | solution.py:36
  449.1 0.0 all-gather.4.cloned.1.call-done
  449.1 23.0 %fusion.9 = f32[5,8,205,512]{3,2,1,0:T(8,128)} fusion(bf16[8,5,205,1536]{3,2,1,0:T(8,128)(2,1)} %all-to-all-done, bf16[5,1536,512]{2,1,0:T(8,128)(2,1)} %all-gather.4.cloned.1.call-done), kind=kOutput, calls=%fused_computation.12 | convolution fusion | flops 12897484800 | bytes 49848320 | tf_op jit(solution)/shard_map/sncd,ndf->sncf/dot_general | solution.py:35
  472.1 0.0 all-gather.8.cloned.1.call-done
  472.1 27.2 %convert_bitcast_fusion = bf16[8,5,205,1536]{3,2,0,1:T(8,128)(2,1)} fusion(f32[5,8,205,512]{3,2,1,0:T(8,128)} %fusion.7, f32[5,8,205,512]{3,2,1,0:T(8,128)} %fusion.9, bf16[5,512,1536]{2,1,0:T(8,128)(2,1)} %all-gather.8.cloned.1.call-done), kind=kOutput, calls=%fused_computation.8 | convolution fusion | flops 12935270400 | bytes 66641920 | tf_op jit(solution)/shard_map/sncf,nfd->sncd/dot_general | solution.py:38
  499.3 12.3 %copy.38 = bf16[8,5,205,1536]{3,2,1,0:T(8,128)(2,1)S(1)} copy(bf16[8,5,205,1536]{3,2,0,1:T(8,128)(2,1)} %convert_bitcast_fusion) | data formatting | bytes 50380800 | tf_op jit(solution)/shard_map/convert_element_type | solution.py:38
  511.6 283.0 %all_to_all.10 = bf16[8,5,205,1536]{3,2,1,0:T(8,128)(2,1)} all-to-all(bf16[8,5,205,1536]{3,2,1,0:T(8,128)(2,1)S(1)} %copy.38), channel_id=1, replica_groups=mesh['rep'=1,'fsdp'=4,'ep'=8] {'ep'}, dimensions={0} | all-to-all | bytes 50380800 | tf_op jit(solution)/shard_map/all_to_all | solution.py:39
  794.6 0.0 copy-start.3
  794.6 0.0 copy-start.4
  794.6 30.9 %reshape.72 = bf16[8200,1536,1]{1,0,2:T(8,128)(2,1)} reshape(bf16[8,5,205,1536]{3,2,1,0:T(8,128)(2,1)} %all_to_all.10) | data formatting | bytes 50380800 | tf_op jit(solution)/shard_map/reshape | solution.py:40
  825.5 0.0 copy-done.3
  825.5 0.0 copy-done.4
  825.5 0.0 copy-start.1
  825.5 113.4 %multiply_reduce_fusion = f32[512,1536]{1,0:T(8,128)S(1)} fusion(bf16[8200,1536,1]{1,0,2:T(8,128)(2,1)} %reshape.72, s32[512,8]{0,1:T(8,128)S(1)} %copy-done.3, f32[512,8]{0,1:T(8,128)S(1)} %copy-done.4), kind=kOutput, calls=%fused_computation.9 | convolution fusion | flops 103225262080 | bytes 28368896 | tf_op jit(solution)/shard_map/tkf,fd->tkd/dot_general | solution.py:41
  939.0 0.0 copy-done.1
  939.0 1.6 add_convert_fusion
  (1 shorter events, 0.0 us)
Async XLA Ops:
  6.5 82.0 %copy-start = (bf16[512,1536]{1,0:T(8,128)(2,1)S(1)}, bf16[512,1536]{1,0:T(8,128)(2,1)}, u32[]{:S(2)}) copy-start(bf16[512,1536]{1,0:T(8,128)(2,1)} %param.6) | copy-start | bytes 4718596
  6.5 143.5 %all-gather.6.cloned.1.call-start = ((), (), s32[]{:S(2)}) async-start(), calls=%async_computation.3 | async-start | bytes 9830400 | tf_op jit(solution)/shard_map/all_gather | solution.py:33
  22.7 86.3 %copy-start.2 = (s32[512,8]{0,1:T(8,128)}, s32[512,8]{0,1:T(8,128)S(1)}, u32[]{:S(2)}) copy-start(s32[512,8]{0,1:T(8,128)S(1)} %copy.34) | copy-start | bytes 49156
  139.9 286.1 %all-to-all-start = ((bf16[8,5,205,1536]{3,2,1,0:T(8,128)(2,1)}), bf16[8,5,205,1536]{3,2,1,0:T(8,128)(2,1)}, u32[]{:S(2)}, u32[]{:S(2)}) async-start(bf16[8,5,205,1536]{3,2,1,0:T(8,128)(2,1)} %reshape.67), calls=%async_computation | async-start | bytes 51118080 | tf_op jit(solution)/shard_map/all_to_all | solution.py:31
  148.4 300.7 %all-gather.4.cloned.1.call-start = ((), (), s32[]{:S(2)}) async-start(), calls=%async_computation.2 | async-start | bytes 9830400 | tf_op jit(solution)/shard_map/all_gather | solution.py:32
  149.2 322.9 %all-gather.8.cloned.1.call-start = ((), (), s32[]{:S(2)}) async-start(), calls=%async_computation.4 | async-start | bytes 9830400 | tf_op jit(solution)/shard_map/all_gather | solution.py:34
  794.6 30.9 %copy-start.3 = (s32[512,8]{0,1:T(8,128)S(1)}, s32[512,8]{0,1:T(8,128)}, u32[]{:S(2)}) copy-start(s32[512,8]{0,1:T(8,128)} %copy-done.2) | copy-start | bytes 49156
  794.6 30.9 %copy-start.4 = (f32[512,8]{0,1:T(8,128)S(1)}, f32[512,8]{0,1:T(8,128)}, u32[]{:S(2)}) copy-start(f32[512,8]{0,1:T(8,128)} %param.8) | copy-start | bytes 49156
  825.5 113.4 %copy-start.1 = (bf16[512,1536]{1,0:T(8,128)(2,1)S(1)}, bf16[512,1536]{1,0:T(8,128)(2,1)}, u32[]{:S(2)}) copy-start(bf16[512,1536]{1,0:T(8,128)(2,1)} %param.6) | copy-start | bytes 4718596
Sparse Core Ops, SparseCore 0:
  8.9 80.0 all-gather.5
  150.8 78.3 all-gather.3
  230.8 77.2 all-gather.7
where the time goes:
time: 948 us; the launch traced here: 947 us
  blocking collectives  283 us (30%)
  waiting for transfers between devices  278 us (29%)
  matrix products  207 us (22%)
  other arithmetic  80.7 us (9%)
  local copies, waits for them, and re-layouts  76.2 us (8%)
  between operations  13.2 us (1%)
    all_to_all x1, blocking collectives, device_step(): back_buf = lax.all_to_all(expert_out, 'ep', 0, 0, tiled=True)  283 us
    all_to_all x1, waiting for transfers between devices, device_step(): recv_buf = lax.all_to_all(send_buf, 'ep', 0, 0, tiled=True)  276 us
    dot_general x1, matrix products, device_step(): jnp.einsum('tkf,fd->tkd', select, back_rows, preferred_element_type=jnp.f...  113 us
    reduce_sum x1, other arithmetic, device_step(): jnp.einsum('tkf,td->fd', select, tokens, preferred_element_type=jnp.float32)  65.8 us
    reshape x1, local copies, waits for them, and re-layouts, device_step(): back_rows = back_buf.reshape(num_experts * capacity, model_dim)  30.9 us
    reshape x1, local copies, waits for them, and re-layouts, device_step(): send_buf = send_buf.reshape(ep_size, n_local, capacity, model_dim)  30.9 us
    dot_general x1, matrix products, device_step(): jnp.einsum('sncf,nfd->sncd', hidden, wd_full, preferred_element_type=jnp....  27.2 us
    dot_general x1, matrix products, device_step(): jnp.einsum('sncd,ndf->sncf', recv_buf, wu_full, preferred_element_type=jn...  23.1 us
  transfers between devices with their start and end apart: 4, of which 1 were waited for; matrix products, arithmetic and copies ran while one was open for 19% of the time, Pallas kernels for 0%

commit v1 on v0

v1 whole, which is shorter than its diff:
```python
import functools

import jax
import jax.numpy as jnp
from jax import lax
from jax.experimental import pallas as pl
from jax.experimental.pallas import tpu as pltpu
from jax.sharding import PartitionSpec as P

MESH = pl.DeviceIdType.MESH
BF16 = jnp.bfloat16
F32 = jnp.float32

RING = 4
CHUNKS = 10
UNITS = 3
PIECES = 6


def moe_kernel(cap, tok_in, idx_ref, gates_ref, wg, wu, wd, out_ref, gu_land, d_land,
               tok, wbuf, hid, wdb, accs, in_a, in_b, in_l, in_r, gsrc, grecv, gcol,
               tload, tsend, trecv, tfar, gsend, grsem,
               ysend, ssend, from_l, from_r, far_a, far_b, from_s,
               dysend, dssend, dfrom_l, dfrom_r, dfar_a, dfar_b, dfrom_s,
               lsem, dlsem, asend, asem, bsem, lsum, rsum):
    rows = tok_in.shape[0]
    half = rows // 2
    n_local, shard, ffn = wg.shape
    fh = ffn // 2
    hs = shard // 2
    top_k = idx_ref.shape[1]
    unit = shard // UNITS

    q = lax.axis_index('fsdp')
    ep = lax.axis_index('ep')
    chip = ep // 2
    core = ep % 2
    q_l, q_r, q_f = (q + 3) % RING, (q + 1) % RING, (q + 2) % RING
    y_r, y_l = {'fsdp': q_r}, {'fsdp': q_l}
    x_r = {'ep': ((chip + 1) % RING) * 2 + core}
    x_l = {'ep': ((chip + 3) % RING) * 2 + core}
    x_f = {'ep': ((chip + 2) % RING) * 2 + core}
    sib = {'ep': chip * 2 + 1 - core}
    mine = core * n_local
    theirs = (1 - core) * n_local

    def wait(ref, sem):
        pltpu.make_async_copy(ref, ref, sem).wait()

    def send(src, dst, ssem, rsem, dev):
        pltpu.make_async_remote_copy(src_ref=src, dst_ref=dst, send_sem=ssem, recv_sem=rsem,
                                     device_id=dev, device_id_type=MESH).start()

    def fcols(f):
        return pl.ds(pl.multiple_of(f * fh, fh), fh)

    def own_gu(n):
        e, f = n // 2, n % 2
        for dev, ssem, rsem in ((y_r, ysend, from_l), (y_l, ysend, from_r), (sib, ssend, from_s)):
            for m, w in enumerate((wg, wu)):
                send(w.at[e, :, fcols(f)], gu_land.at[mine + e, f, q, m], ssem.at[n], rsem.at[n], dev)

    def fwd_gu(n):
        e, f = n // 2, n % 2
        lref = gu_land.at[mine + e, f, q_l]
        rref = gu_land.at[mine + e, f, q_r]
        wait(lref, from_l.at[n])
        la = gu_land.at[mine + e, f, q_l, :, 0:hs, :]
        send(la, la, ysend.at[n], far_a.at[n], y_r)
        wait(rref, from_r.at[n])
        rb = gu_land.at[mine + e, f, q_r, :, hs:shard, :]
        send(rb, rb, ysend.at[n], far_b.at[n], y_l)
        send(lref, lref, ssend.at[n], from_s.at[n], sib)
        send(rref, rref, ssend.at[n], from_s.at[n], sib)

    def far_gu(n):
        e, f = n // 2, n % 2
        wait(gu_land.at[mine + e, f, q_f, :, 0:hs, :], far_a.at[n])
        wait(gu_land.at[mine + e, f, q_f, :, hs:shard, :], far_b.at[n])
        fref = gu_land.at[mine + e, f, q_f]
        send(fref, fref, ssend.at[n], from_s.at[n], sib)

    def own_d():
        for dev, ssem, rsem in ((y_r, dysend, dfrom_l), (y_l, dysend, dfrom_r)):
            for j in range(UNITS):
                send(wd.at[:, :, j * unit:(j + 1) * unit], d_land.at[q * UNITS + j, pl.ds(mine, n_local)],
                     ssem.at[j], rsem.at[j], dev)

    def own_d_sib():
        for j in range(UNITS):
            send(wd.at[:, :, j * unit:(j + 1) * unit], d_land.at[q * UNITS + j, pl.ds(mine, n_local)],
                 dssend.at[j], dfrom_s.at[0, j], sib)

    def fwd_d(j):
        lref = d_land.at[q_l * UNITS + j, pl.ds(mine, n_local)]
        rref = d_land.at[q_r * UNITS + j, pl.ds(mine, n_local)]
        wait(lref, dfrom_l.at[j])
        la = d_land.at[q_l * UNITS + j, pl.ds(mine, n_local), 0:fh]
        send(la, la, dysend.at[j], dfar_a.at[j], y_r)
        wait(rref, dfrom_r.at[j])
        rb = d_land.at[q_r * UNITS + j, pl.ds(mine, n_local), fh:ffn]
        send(rb, rb, dysend.at[j], dfar_b.at[j], y_l)
        send(lref, lref, dssend.at[j], dfrom_s.at[1, j], sib)
        send(rref, rref, dssend.at[j], dfrom_s.at[2, j], sib)

    def far_d(j):
        wait(d_land.at[q_f * UNITS + j, pl.ds(mine, n_local), 0:fh], dfar_a.at[j])
        wait(d_land.at[q_f * UNITS + j, pl.ds(mine, n_local), fh:ffn], dfar_b.at[j])
        fref = d_land.at[q_f * UNITS + j, pl.ds(mine, n_local)]
        send(fref, fref, dssend.at[j], dfrom_s.at[3, j], sib)

    def load_mine(n):
        e, f = n // 2, n % 2
        for m, w in enumerate((wg, wu)):
            pltpu.make_async_copy(w.at[e, :, fcols(f)], wbuf.at[0, q, :, m * fh:(m + 1) * fh], lsem.at[0]).start()
            for other in (q_l, q_r, q_f):
                pltpu.make_async_copy(gu_land.at[mine + e, f, other, m],
                                      wbuf.at[0, other, :, m * fh:(m + 1) * fh], lsem.at[0]).start()

    def load_theirs(n):
        e, f = n // 2, n % 2
        wait(gu_land.at[theirs + e, f], from_s.at[n])
        for m in range(2):
            pltpu.make_async_copy(gu_land.at[theirs + e, f, :, m],
                                  wbuf.at[1, :, :, m * fh:(m + 1) * fh], lsem.at[1]).start()

    def seq_unit(s):
        if s < 3:
            return 0, s
        if s < 9:
            return (1 if s % 2 else 2), (s - 3) // 2
        return 3, s - 9

    shards = (q, q_l, q_r, q_f)

    def load_piece(p):
        for i in range(2):
            kind, j = seq_unit(2 * p + i)
            gid = shards[kind] * UNITS + j
            lanes = slice(i * unit, (i + 1) * unit)
            wait(d_land.at[gid, pl.ds(theirs, n_local)], dfrom_s.at[kind, j])
            if kind == 0:
                pltpu.make_async_copy(wd.at[:, :, j * unit:(j + 1) * unit],
                                      wdb.at[p % 2, pl.ds(mine, n_local), :, lanes], dlsem.at[p % 2]).start()
                pltpu.make_async_copy(d_land.at[gid, pl.ds(theirs, n_local)],
                                      wdb.at[p % 2, pl.ds(theirs, n_local), :, lanes], dlsem.at[p % 2]).start()
            else:
                pltpu.make_async_copy(d_land.at[gid], wdb.at[p % 2, :, :, lanes], dlsem.at[p % 2]).start()

    barrier = pltpu.get_barrier_semaphore()
    for dev in (y_r, y_l, x_r, x_l, x_f, sib):
        pl.semaphore_signal(barrier, inc=1, device_id=dev, device_id_type=MESH)
    pl.semaphore_wait(barrier, 6)

    own_tok = pltpu.make_async_copy(tok_in, tok.at[0], tload)
    own_tok.start()
    send(tok_in, tok.at[1], tsend.at[0], trecv.at[0], x_r)
    send(tok_in, tok.at[2], tsend.at[1], trecv.at[1], x_l)
    own_gu(0)
    own_gu(1)
    own_d_sib()

    lane = lax.broadcasted_iota(jnp.int32, (rows, 128), 1)
    chosen = jnp.zeros((rows, 128), F32)
    gval = jnp.zeros((rows, 128), F32)
    for j in range(top_k):
        hit = idx_ref[:, j:j + 1] == lane
        chosen = jnp.where(hit, 1.0, chosen)
        gval = jnp.where(hit, gates_ref[:, j:j + 1], gval)
    earlier = lax.broadcasted_iota(jnp.int32, (rows, rows), 1) < lax.broadcasted_iota(jnp.int32, (rows, rows), 0)
    before = jnp.dot(jnp.where(earlier, 1.0, 0.0).astype(BF16), chosen.astype(BF16), preferred_element_type=F32)
    gsrc[...] = jnp.where(before < cap - 0.5, gval, 0.0)

    fwd_gu(0)
    own_gu(2)
    fwd_gu(1)
    own_gu(3)
    far_gu(0)
    fwd_gu(2)
    own_gu(4)
    wait(tok.at[1], trecv.at[0])
    ta = tok.at[1, 0:half]
    send(ta, tok.at[3, 0:half], tsend.at[2], tfar.at[0], x_r)
    wait(tok.at[2], trecv.at[1])
    tb = tok.at[2, half:rows]
    send(tb, tok.at[3, half:rows], tsend.at[3], tfar.at[1], x_l)
    for i, dev in enumerate((x_r, x_l, x_f)):
        send(gsrc, grecv.at[i], gsend.at[i], grsem.at[i], dev)
    far_gu(1)
    fwd_gu(3)
    own_gu(5)
    far_gu(2)
    own_tok.wait()
    load_mine(0)
    wait(tok.at[3, 0:half], tfar.at[0])
    wait(tok.at[3, half:rows], tfar.at[1])

    def gu_unit(u, slot, n):
        e, f = n // 2, n % 2
        base = jnp.where(slot == 0, mine, theirs)

        def block(b, carry):
            both = jnp.dot(tok[b], wbuf[slot].reshape(RING * shard, ffn), preferred_element_type=F32)
            act_a, act_b = both[:, :fh], both[:, fh:]
            hid[base + e, b, :, fcols(f)] = (act_a * jax.nn.sigmoid(act_a) * act_b).astype(BF16)
            return carry
        return block

    def unit_step(u, carry):
        n, slot = u // 2, u % 2
        wait(wbuf.at[slot], lsem.at[slot])
        block = gu_unit(u, slot, n)
        lax.fori_loop(0, 2, block, 0)

        @pl.when((u % 3 == 1) & (u <= 16))
        def _():
            fwd_gu(4 + u // 3)

            @pl.when(u <= 10)
            def _():
                own_gu(6 + u // 3)

            @pl.when(u == 16)
            def _():
                own_d()

        for k, step in ((3, 2), (4, 5), (5, 8), (6, 11), (7, 13), (8, 15), (9, 17)):
            @pl.when(u == step)
            def _(k=k):
                far_gu(k)

        @pl.when(slot == 0)
        def _():
            load_theirs(n)

        @pl.when((slot == 1) & (n < CHUNKS - 1))
        def _():
            load_mine(n + 1)

        @pl.when(u == 18)
        def _():
            load_piece(0)

        lax.fori_loop(2, 4, block, 0)
        return carry

    lax.fori_loop(0, 2 * CHUNKS, unit_step, 0)

    shift = (128 - chip * 2 * n_local) % 128
    gcol[0] = pltpu.roll(gsrc[...], shift, 1)
    for i in range(3):
        wait(grecv.at[i], grsem.at[i])
        gcol[i + 1] = pltpu.roll(grecv[i], shift, 1)

    def finish(p):
        s = p % 2
        wait(in_l.at[p], lsum.at[p])
        wait(in_r.at[p], rsum.at[p])
        for i in range(2):
            if isinstance(p, int):
                kind, j = seq_unit(2 * p + i)
                gid = shards[kind] * UNITS + j
            else:
                sq = 2 * p + i
                mid = sq - 3
                kind = jnp.where(sq < 3, 0, jnp.where(sq < 9, 1 + mid % 2, 3))
                j = jnp.where(sq < 3, sq, jnp.where(sq < 9, mid // 2, sq - 9))
                sh = jnp.where(kind == 0, q, jnp.where(kind == 1, q_l, jnp.where(kind == 2, q_r, q_f)))
                gid = sh * UNITS + j
            cols = pl.ds(pl.multiple_of(gid * unit, unit), unit)
            lanes = slice(i * unit, (i + 1) * unit)
            total = accs[s, 3, :, lanes] + in_l[p, :, lanes] + in_r[p, :, lanes]
            out_ref[:, cols] = (tok[0, :, cols].astype(F32) + total).astype(BF16)

    def block_step(t, carry):
        p, i = t // 4, t % 4
        s = p % 2
        b = 3 - i

        @pl.when(i == 0)
        def _():
            wait(wdb.at[s], dlsem.at[s])

        @pl.when((p >= 2) & (i < 3))
        def _():
            wait(accs.at[s, i], asend.at[p - 2, i])

        gates_b = gcol[b]
        total = None
        for e in range(2 * n_local):
            o = jnp.dot(hid[e, b], wdb[s, e], preferred_element_type=F32).astype(BF16).astype(F32)
            g = gates_b[:, e:e + 1]
            o = jnp.where(g != 0.0, g * o, 0.0)
            total = o if total is None else total + o
        accs[s, i] = total

        @pl.when(i == 0)
        def _():
            send(accs.at[s, 0, 0:half], in_a.at[p], asend.at[p, 0], asem.at[p], x_r)
            send(accs.at[s, 0, half:rows], in_b.at[p], asend.at[p, 0], bsem.at[p], x_l)

            @pl.when(p == 1)
            def _():
                fwd_d(1)

            @pl.when(p == 2)
            def _():
                fwd_d(2)

            @pl.when(p == 3)
            def _():
                far_d(0)

            @pl.when(p == 4)
            def _():
                far_d(1)
                far_d(2)

        @pl.when(i == 1)
        def _():
            send(accs.at[s, 1, half:rows], in_l.at[p, half:rows], asend.at[p, 1], lsum.at[p], x_r)

        @pl.when(i == 2)
        def _():
            send(accs.at[s, 2, 0:half], in_r.at[p, 0:half], asend.at[p, 2], rsum.at[p], x_l)
            wait(in_a.at[p], asem.at[p])
            accs[s, 1, 0:half] += in_a[p]
            send(accs.at[s, 1, 0:half], in_l.at[p, 0:half], asend.at[p, 1], lsum.at[p], x_r)
            wait(in_b.at[p], bsem.at[p])
            accs[s, 2, half:rows] += in_b[p]
            send(accs.at[s, 2, half:rows], in_r.at[p, half:rows], asend.at[p, 2], rsum.at[p], x_l)

            @pl.when(p == 0)
            def _():
                fwd_d(0)

            for k in range(1, PIECES):
                @pl.when(p == k - 1)
                def _(k=k):
                    load_piece(k)

        @pl.when((i == 3) & (p >= 1))
        def _():
            finish(p - 1)
        return carry

    lax.fori_loop(0, 4 * PIECES, block_step, 0)
    finish(PIECES - 1)

    def drain(n, carry):
        wait(gu_land.at[0, 0, 0:3], ysend.at[n])
        wait(gu_land.at[0, 0], ssend.at[n])
        return carry

    lax.fori_loop(0, CHUNKS, drain, 0)
    for j in range(UNITS):
        wait(d_land.at[0:3, 0:n_local], dysend.at[j])
        wait(d_land.at[0:4, 0:n_local], dssend.at[j])
    wait(tok.at[1], tsend.at[0])
    wait(tok.at[1], tsend.at[1])
    wait(tok.at[1, 0:half], tsend.at[2])
    wait(tok.at[1, 0:half], tsend.at[3])
    for i in range(3):
        wait(gsrc, gsend.at[i])
    for p in (PIECES - 2, PIECES - 1):
        for i in range(3):
            wait(accs.at[0, 0], asend.at[p, i])


def solution(mesh):
    ep_size = mesh.shape['ep']
    row_spec = P(('rep', 'ep', 'fsdp'), None)

    def device_step(tokens, expert_idx, gates, w_gate, w_up, w_down):
        rows, top_k = expert_idx.shape
        n_local, shard, ffn = w_gate.shape
        model_dim = tokens.shape[1]
        num_experts = n_local * ep_size
        cap = (2 * rows * top_k + num_experts - 1) // num_experts
        fh, half, unit = ffn // 2, rows // 2, shard // UNITS
        piece = 2 * unit
        vmem = pl.BlockSpec(memory_space=pltpu.VMEM)
        hbm = pl.BlockSpec(memory_space=pl.ANY)
        dma = pltpu.SemaphoreType.DMA
        out, _, _ = pl.pallas_call(
            functools.partial(moe_kernel, cap),
            out_shape=(
                jax.ShapeDtypeStruct((rows, model_dim), BF16),
                jax.ShapeDtypeStruct((2 * n_local, 2, RING, 2, shard, fh), BF16),
                jax.ShapeDtypeStruct((RING * UNITS, 2 * n_local, ffn, unit), BF16),
            ),
            in_specs=[hbm, vmem, vmem, hbm, hbm, hbm],
            out_specs=(vmem, hbm, hbm),
            scratch_shapes=[
                pltpu.VMEM((4, rows, model_dim), BF16),
                pltpu.VMEM((2, RING, shard, ffn), BF16),
                pltpu.VMEM((2 * n_local, 4, rows, ffn), BF16),
                pltpu.VMEM((2, 2 * n_local, ffn, piece), BF16),
                pltpu.VMEM((2, 4, rows, piece), F32),
                pltpu.VMEM((PIECES, half, piece), F32),
                pltpu.VMEM((PIECES, half, piece), F32),
                pltpu.VMEM((PIECES, rows, piece), F32),
                pltpu.VMEM((PIECES, rows, piece), F32),
                pltpu.VMEM((rows, 128), F32),
                pltpu.VMEM((3, rows, 128), F32),
                pltpu.VMEM((4, rows, 128), F32),
                dma, dma((4,)), dma((2,)), dma((2,)), dma((3,)), dma((3,)),
                dma((CHUNKS,)), dma((CHUNKS,)), dma((CHUNKS,)), dma((CHUNKS,)), dma((CHUNKS,)), dma((CHUNKS,)), dma((CHUNKS,)),
                dma((UNITS,)), dma((UNITS,)), dma((UNITS,)), dma((UNITS,)), dma((UNITS,)), dma((UNITS,)), dma((4, UNITS)),
                dma((2,)), dma((2,)), dma((PIECES, 3)), dma((PIECES,)), dma((PIECES,)), dma((PIECES,)), dma((PIECES,)),
            ],
            compiler_params=pltpu.CompilerParams(collective_id=0, has_side_effects=True, vmem_limit_bytes=67043328),
            name='moe_ring',
        )(tokens, expert_idx, gates, w_gate, w_up, w_down)
        return out

    return jax.shard_map(device_step, mesh=mesh, in_specs=(row_spec, row_spec, row_spec, P('ep', 'fsdp', None), P('ep', 'fsdp', None), P('ep', None, 'fsdp')), out_specs=row_spec, check_vma=False)
```

time: 948 us -> 265 us (0.28)
  blocking collectives: 283 us -> 0 us
  waiting for transfers between devices: 278 us -> 0 us
  Pallas kernels: 0 us -> 259 us
  matrix products: 207 us -> 0 us
  other arithmetic: 80.7 us -> 0 us
  local copies, waits for them, and re-layouts: 76.2 us -> 5.79 us
  between operations: 13.2 us -> 0.01 us
    all_to_all x1 -> x0, blocking collectives: 283 us -> none  [device_step(): back_buf = lax.all_to_all(expert_out, 'ep', 0, 0, tiled=True)]
    all_to_all x1 -> x0, waiting for transfers between devices: 276 us -> none  [device_step(): recv_buf = lax.all_to_all(send_buf, 'ep', 0, 0, tiled=True)]
    pallas_call x0 -> x1, Pallas kernels: none -> 259 us  [device_step(): pl.pallas_call(functools.partial(moe_kernel, cap), out_shape=(jax.ShapeDt...]
    dot_general x5 -> x0, matrix products: 207 us -> none  [the longest x1 113 us: device_step(): jnp.einsum('tkf,fd->tkd', select, back_rows, preferred_element_type=jnp.f...]
    reduce_sum x2 -> x0, other arithmetic: 66.3 us -> none  [the longest x1 65.8 us: device_step(): jnp.einsum('tkf,td->fd', select, tokens, preferred_element_type=jnp.float32)]
    reshape x2 -> x0, local copies, waits for them, and re-layouts: 61.8 us -> none  [the longest x1 30.9 us: device_step(): back_rows = back_buf.reshape(num_experts * capacity, model_dim)]
    convert_element_type x1 -> x0, local copies, waits for them, and re-layouts: 12.3 us -> none  [device_step(): jnp.einsum('sncf,nfd->sncd', hidden, wd_full, preferred_element_type=jnp....]
    another operation x3 -> x0, other arithmetic: 12 us -> none
  transfers between devices with their start and end apart: 4 -> 0, of which waited for: 1 -> 0; matrix products, arithmetic and copies ran while one was open for 19% -> 0% of each run, Pallas kernels for 0% -> 0%
where the time goes in v1:
time: 265 us
  Pallas kernels  259 us (98%)
  local copies, waits for them, and re-layouts  5.79 us (2%)
    pallas_call x1, Pallas kernels, device_step(): pl.pallas_call(functools.partial(moe_kernel, cap), out_shape=(jax.ShapeDt...  259 us
    unnamed x3, local copies, waits for them, and re-layouts  5.79 us

profile of v1, /device:TPU:97, one launch (start us, length us, event | category | flops | bytes accessed | tf_op | source)
XLA Modules:
  0.0 265.1 jit_solution(3105911976225254715)
XLA Ops:
  0.0 1.6 copy.7.idx_ref
  1.6 1.6 copy.8.gates_ref
  3.1 259.3 %moe_ring.1 = (bf16[512,1536]{1,0:T(8,128)(2,1)}, bf16[10,2,4,2,384,256]{5,4,3,2,1,0:T(8,128)(2,1)}, bf16[12,10,512,128]{3,2,1,0:T(8,128)(2,1)}) custom-call(bf16[512,1536]{1,0:T(8,128)(2,1)} %tok_in.1, s32[512,8]{1,0:T(8,128)} %copy.7.idx_ref, f32[512,8]{1,0:T(8,128)} %copy.8.gates_ref, bf16[5,384,512]{2,1,0:T(8,128)(2,1)} %wg.1, bf16[5,384,512]{2,1,0:T(8,128)(2,1)} %wu.1, ...), custom_call_target="tpu_custom_call" | custom-call | tf_op jit(solution)/shard_map/moe_ring/pallas_call | solution.py:385
  262.4 2.7 %copy.10 = bf16[512,1536]{1,0:T(8,128)(2,1)} copy(bf16[512,1536]{1,0:T(8,128)(2,1)} %get-tuple-element.6) | data formatting | bytes 3145728

commit v2 on v1

--- a/solution.py
+++ b/solution.py
@@ -18,17 +18,17 @@
 
 
 def moe_kernel(cap, tok_in, idx_ref, gates_ref, wg, wu, wd, out_ref, gu_land, d_land,
-               tok, wbuf, hid, wdb, accs, in_a, in_b, in_l, in_r, gsrc, grecv, gcol,
+               tok, wbuf, hid, wdb, wlast, accs, in_a, in_b, in_l, in_r, gsrc, grecv, gcol, stage,
                tload, tsend, trecv, tfar, gsend, grsem,
                ysend, ssend, from_l, from_r, far_a, far_b, from_s,
                dysend, dssend, dfrom_l, dfrom_r, dfar_a, dfar_b, dfrom_s,
-               lsem, dlsem, asend, asem, bsem, lsum, rsum):
+               lsem, dlsem, asend, asem, bsem, lsum, rsum, osem, efwd):
     rows = tok_in.shape[0]
     half = rows // 2
     n_local, shard, ffn = wg.shape
     fh = ffn // 2
     hs = shard // 2
-    top_k = idx_ref.shape[1]
+    top_k = idx_ref.shape[0]
     unit = shard // UNITS
 
     q = lax.axis_index('fsdp')
@@ -80,6 +80,41 @@
         fref = gu_land.at[mine + e, f, q_f]
         send(fref, fref, ssend.at[n], from_s.at[n], sib)
 
+    last = CHUNKS - 1
+    le, lf = last // 2, last % 2
+    top, low = slice(0, hs), slice(hs, shard)
+
+    def to_sib_last(shard_id, ref):
+        for m in range(2):
+            send(ref(m), wlast.at[shard_id, :, m * fh:(m + 1) * fh], ssend.at[last], from_s.at[last], sib)
+
+    def own_last():
+        for dev, order, early, late in ((y_r, (top, low), 0, from_l), (y_l, (low, top), 1, from_r)):
+            for part, rsem in zip(order, (efwd.at[early], late.at[last])):
+                for m, w in enumerate((wg, wu)):
+                    send(w.at[le, part, lf * fh:(lf + 1) * fh], gu_land.at[mine + le, lf, q, m, part],
+                         ysend.at[last], rsem, dev)
+        to_sib_last(q, lambda m: (wg, wu)[m].at[le, :, lf * fh:(lf + 1) * fh])
+
+    def fwd_last():
+        la = gu_land.at[mine + le, lf, q_l, :, top]
+        wait(la, efwd.at[0])
+        send(la, la, ysend.at[last], far_a.at[last], y_r)
+        rb = gu_land.at[mine + le, lf, q_r, :, low]
+        wait(rb, efwd.at[1])
+        send(rb, rb, ysend.at[last], far_b.at[last], y_l)
+
+    def near_last():
+        wait(gu_land.at[mine + le, lf, q_l, :, low], from_l.at[last])
+        to_sib_last(q_l, lambda m: gu_land.at[mine + le, lf, q_l, m])
+        wait(gu_land.at[mine + le, lf, q_r, :, top], from_r.at[last])
+        to_sib_last(q_r, lambda m: gu_land.at[mine + le, lf, q_r, m])
+
+    def far_last():
+        wait(gu_land.at[mine + le, lf, q_f, :, top], far_a.at[last])
+        wait(gu_land.at[mine + le, lf, q_f, :, low], far_b.at[last])
+        to_sib_last(q_f, lambda m: gu_land.at[mine + le, lf, q_f, m])
+
     def own_d():
         for dev, ssem, rsem in ((y_r, dysend, dfrom_l), (y_l, dysend, dfrom_r)):
             for j in range(UNITS):
@@ -110,19 +145,24 @@
         send(fref, fref, dssend.at[j], dfrom_s.at[3, j], sib)
 
     def load_mine(n):
-        e, f = n // 2, n % 2
+        e, f, par = n // 2, n % 2, n % 2
         for m, w in enumerate((wg, wu)):
-            pltpu.make_async_copy(w.at[e, :, fcols(f)], wbuf.at[0, q, :, m * fh:(m + 1) * fh], lsem.at[0]).start()
+            lanes = slice(m * fh, (m + 1) * fh)
+            pltpu.make_async_copy(w.at[e, :, fcols(f)], wbuf.at[par, 0, q, :, lanes], lsem.at[par, 0]).start()
             for other in (q_l, q_r, q_f):
                 pltpu.make_async_copy(gu_land.at[mine + e, f, other, m],
-                                      wbuf.at[0, other, :, m * fh:(m + 1) * fh], lsem.at[0]).start()
-
-    def load_theirs(n):
-        e, f = n // 2, n % 2
-        wait(gu_land.at[theirs + e, f], from_s.at[n])
+                                      wbuf.at[par, 0, other, :, lanes], lsem.at[par, 0]).start()
+
+    def load_theirs(n, again=False):
+        e, f, par = n // 2, n % 2, n % 2
+        if not again:
+            wait(gu_land.at[theirs + e, f], from_s.at[n])
         for m in range(2):
             pltpu.make_async_copy(gu_land.at[theirs + e, f, :, m],
-                                  wbuf.at[1, :, :, m * fh:(m + 1) * fh], lsem.at[1]).start()
+                                  wbuf.at[par, 1, :, :, m * fh:(m + 1) * fh], lsem.at[par, 1]).start()
+
+    def loaded(n, side):
+        wait(wbuf.at[n % 2, side], lsem.at[n % 2, side])
 
     def seq_unit(s):
         if s < 3:
@@ -160,22 +200,24 @@
     own_gu(1)
     own_d_sib()
 
-    lane = lax.broadcasted_iota(jnp.int32, (rows, 128), 1)
-    chosen = jnp.zeros((rows, 128), F32)
-    gval = jnp.zeros((rows, 128), F32)
+    expert = lax.broadcasted_iota(jnp.int32, (128, rows), 0)
+    chosen = jnp.zeros((128, rows), F32)
+    gval = jnp.zeros((128, rows), F32)
     for j in range(top_k):
-        hit = idx_ref[:, j:j + 1] == lane
+        hit = idx_ref[j:j + 1, :] == expert
         chosen = jnp.where(hit, 1.0, chosen)
-        gval = jnp.where(hit, gates_ref[:, j:j + 1], gval)
-    earlier = lax.broadcasted_iota(jnp.int32, (rows, rows), 1) < lax.broadcasted_iota(jnp.int32, (rows, rows), 0)
-    before = jnp.dot(jnp.where(earlier, 1.0, 0.0).astype(BF16), chosen.astype(BF16), preferred_element_type=F32)
-    gsrc[...] = jnp.where(before < cap - 0.5, gval, 0.0)
+        gval = jnp.where(hit, gates_ref[j:j + 1, :], gval)
+    earlier = lax.broadcasted_iota(jnp.int32, (rows, rows), 0) < lax.broadcasted_iota(jnp.int32, (rows, rows), 1)
+    before = jnp.dot(chosen.astype(BF16), jnp.where(earlier, 1.0, 0.0).astype(BF16), preferred_element_type=F32)
+    gsrc[...] = jnp.where(before < cap - 0.5, gval, 0.0).T
 
     fwd_gu(0)
     own_gu(2)
     fwd_gu(1)
     own_gu(3)
     far_gu(0)
+    load_mine(0)
+    load_theirs(0)
     fwd_gu(2)
     own_gu(4)
     wait(tok.at[1], trecv.at[0])
@@ -187,70 +229,126 @@
     for i, dev in enumerate((x_r, x_l, x_f)):
         send(gsrc, grecv.at[i], gsend.at[i], grsem.at[i], dev)
     far_gu(1)
-    fwd_gu(3)
-    own_gu(5)
-    far_gu(2)
+    load_mine(1)
+    load_theirs(1)
     own_tok.wait()
-    load_mine(0)
+
+    def gu_item(n, side, b, weights=None):
+        e, f, par = n // 2, n % 2, n % 2
+        w = wbuf[par, side] if weights is None else weights[...]
+        both = jnp.dot(tok[b], w.reshape(RING * shard, ffn), preferred_element_type=F32)
+        act_a, act_b = both[:, :fh], both[:, fh:]
+        base = jnp.where(side == 0, mine, theirs)
+        hid[base + e, b, :, fcols(f)] = (act_a * jax.nn.sigmoid(act_a) * act_b).astype(BF16)
+
+    def gu_items(n, side, b0, b1):
+        def body(b, carry):
+            gu_item(n, side, b)
+            return carry
+        lax.fori_loop(b0, b1, body, 0)
+
+    def early(n, carry):
+        def side_step(side, c):
+            loaded(n, side)
+            gu_items(n, side, 0, 3)
+
+            @pl.when((n == 0) & (side == 1))
+            def _():
+                fwd_gu(3)
+                own_gu(5)
+
+            @pl.when((n == 1) & (side == 0))
+            def _():
+                far_gu(2)
+                load_mine(2)
+
+            @pl.when((n == 1) & (side == 1))
+            def _():
+                load_theirs(2)
+            return c
+        lax.fori_loop(0, 2, side_step, 0)
+        return carry
+
+    lax.fori_loop(0, 3, early, 0)
     wait(tok.at[3, 0:half], tfar.at[0])
     wait(tok.at[3, half:rows], tfar.at[1])
 
-    def gu_unit(u, slot, n):
-        e, f = n // 2, n % 2
-        base = jnp.where(slot == 0, mine, theirs)
-
-        def block(b, carry):
-            both = jnp.dot(tok[b], wbuf[slot].reshape(RING * shard, ffn), preferred_element_type=F32)
-            act_a, act_b = both[:, :fh], both[:, fh:]
-            hid[base + e, b, :, fcols(f)] = (act_a * jax.nn.sigmoid(act_a) * act_b).astype(BF16)
-            return carry
-        return block
-
-    def unit_step(u, carry):
-        n, slot = u // 2, u % 2
-        wait(wbuf.at[slot], lsem.at[slot])
-        block = gu_unit(u, slot, n)
-        lax.fori_loop(0, 2, block, 0)
-
-        @pl.when((u % 3 == 1) & (u <= 16))
-        def _():
-            fwd_gu(4 + u // 3)
-
-            @pl.when(u <= 10)
-            def _():
-                own_gu(6 + u // 3)
-
-            @pl.when(u == 16)
-            def _():
-                own_d()
-
-        for k, step in ((3, 2), (4, 5), (5, 8), (6, 11), (7, 13), (8, 15), (9, 17)):
-            @pl.when(u == step)
-            def _(k=k):
-                far_gu(k)
-
-        @pl.when(slot == 0)
-        def _():
-            load_theirs(n)
-
-        @pl.when((slot == 1) & (n < CHUNKS - 1))
-        def _():
+    def late(k, carry):
+        n, side = 2 - k // 2, k % 2
+
+        @pl.when(n == 0)
+        def _():
+            loaded(n, side)
+        gu_item(n, side, 3)
+
+        @pl.when(k == 1)
+        def _():
+            load_mine(0)
+            load_theirs(0, again=True)
+            fwd_gu(4)
+            own_gu(6)
+
+        @pl.when(k == 4)
+        def _():
+            far_gu(3)
+            load_mine(3)
+        return carry
+
+    lax.fori_loop(0, 6, late, 0)
+    load_theirs(3)
+
+    def steady(n, carry):
+        loaded(n, 0)
+        gu_items(n, 0, 0, 4)
+
+        @pl.when(n == CHUNKS - 2)
+        def _():
+            near_last()
+            own_d()
+            load_piece(0)
+
+        loaded(n, 1)
+        gu_items(n, 1, 0, 2)
+
+        @pl.when(n <= CHUNKS - 4)
+        def _():
+            fwd_gu(n + 2)
+
+            @pl.when(n <= 4)
+            def _():
+                own_gu(n + 4)
+
+            @pl.when(n == CHUNKS - 4)
+            def _():
+                own_last()
+
+        @pl.when(n <= CHUNKS - 3)
+        def _():
+            far_gu(n + 1)
             load_mine(n + 1)
 
-        @pl.when(u == 18)
-        def _():
-            load_piece(0)
-
-        lax.fori_loop(2, 4, block, 0)
+        gu_items(n, 1, 2, 4)
+
+        @pl.when(n <= CHUNKS - 3)
+        def _():
+            load_theirs(n + 1)
+
+        @pl.when(n == CHUNKS - 3)
+        def _():
+            fwd_last()
+
+        @pl.when(n == 5)
+        def _():
+            shift = (128 - chip * 2 * n_local) % 128
+            gcol[0] = pltpu.roll(gsrc[...], shift, 1)
+            for i in range(3):
+                wait(grecv.at[i], grsem.at[i])
+                gcol[i + 1] = pltpu.roll(grecv[i], shift, 1)
         return carry
 
-    lax.fori_loop(0, 2 * CHUNKS, unit_step, 0)
-
-    shift = (128 - chip * 2 * n_local) % 128
-    gcol[0] = pltpu.roll(gsrc[...], shift, 1)
-    for i in range(3):
-        wait(grecv.at[i], grsem.at[i])
-        gcol[i + 1] = pltpu.roll(grecv[i], shift, 1)
+    lax.fori_loop(3, CHUNKS - 1, steady, 0)
+    far_last()
+    load_mine(last)
 
     def finish(p):
         s = p % 2
@@ -270,14 +368,31 @@
             cols = pl.ds(pl.multiple_of(gid * unit, unit), unit)
             lanes = slice(i * unit, (i + 1) * unit)
             total = accs[s, 3, :, lanes] + in_l[p, :, lanes] + in_r[p, :, lanes]
-            out_ref[:, cols] = (tok[0, :, cols].astype(F32) + total).astype(BF16)
+            stage[:, cols] = (tok[0, :, cols].astype(F32) + total).astype(BF16)
+            pltpu.make_async_copy(stage.at[:, cols], out_ref.at[:, cols], osem.at[p]).start()
+
+    last_experts = (le, n_local + le)
+    early_experts = [e for e in range(2 * n_local) if e not in last_experts]
+
+    def combine(s, b, experts):
+        gates_b = gcol[b]
+        total = None
+        for e in experts:
+            o = jnp.dot(hid[e, b], wdb[s, e], preferred_element_type=F32).astype(BF16).astype(F32)
+            g = gates_b[:, e:e + 1]
+            o = jnp.where(g != 0.0, g * o, 0.0)
+            total = o if total is None else total + o
+        return total
+
+    wait(wdb.at[0], dlsem.at[0])
+    accs[0, 0] = combine(0, 3, early_experts)
 
     def block_step(t, carry):
         p, i = t // 4, t % 4
         s = p % 2
         b = 3 - i
 
-        @pl.when(i == 0)
+        @pl.when((i == 0) & (p > 0))
         def _():
             wait(wdb.at[s], dlsem.at[s])
 
@@ -285,14 +400,26 @@
         def _():
             wait(accs.at[s, i], asend.at[p - 2, i])
 
-        gates_b = gcol[b]
-        total = None
-        for e in range(2 * n_local):
-            o = jnp.dot(hid[e, b], wdb[s, e], preferred_element_type=F32).astype(BF16).astype(F32)
-            g = gates_b[:, e:e + 1]
-            o = jnp.where(g != 0.0, g * o, 0.0)
-            total = o if total is None else total + o
-        accs[s, i] = total
+        @pl.when(p == 0)
+        def _():
+            @pl.when(i > 0)
+            def _():
+                accs[0, i] = combine(0, b, early_experts)
+
+            @pl.when(i == 0)
+            def _():
+                loaded(last, 0)
+            gu_item(last, 0, b)
+
+            @pl.when(i == 0)
+            def _():
+                wait(wlast, from_s.at[last])
+            gu_item(last, 1, b, wlast)
+            accs[0, i] += combine(0, b, last_experts)
+
+        @pl.when(p > 0)
+        def _():
+            accs[s, i] = combine(s, b, range(2 * n_local))
 
         @pl.when(i == 0)
         def _():
@@ -365,6 +492,8 @@
     for p in (PIECES - 2, PIECES - 1):
         for i in range(3):
             wait(accs.at[0, 0], asend.at[p, i])
+    for p in range(PIECES):
+        wait(stage.at[:, 0:2 * unit], osem.at[p])
 
 
 def solution(mesh):
@@ -390,12 +519,13 @@
                 jax.ShapeDtypeStruct((RING * UNITS, 2 * n_local, ffn, unit), BF16),
             ),
             in_specs=[hbm, vmem, vmem, hbm, hbm, hbm],
-            out_specs=(vmem, hbm, hbm),
+            out_specs=(hbm, hbm, hbm),
             scratch_shapes=[
                 pltpu.VMEM((4, rows, model_dim), BF16),
-                pltpu.VMEM((2, RING, shard, ffn), BF16),
+                pltpu.VMEM((2, 2, RING, shard, ffn), BF16),
                 pltpu.VMEM((2 * n_local, 4, rows, ffn), BF16),
                 pltpu.VMEM((2, 2 * n_local, ffn, piece), BF16),
+                pltpu.VMEM((RING, shard, ffn), BF16),
                 pltpu.VMEM((2, 4, rows, piece), F32),
                 pltpu.VMEM((PIECES, half, piece), F32),
                 pltpu.VMEM((PIECES, half, piece), F32),
@@ -404,14 +534,15 @@
                 pltpu.VMEM((rows, 128), F32),
                 pltpu.VMEM((3, rows, 128), F32),
                 pltpu.VMEM((4, rows, 128), F32),
+                pltpu.VMEM((rows, model_dim), BF16),
                 dma, dma((4,)), dma((2,)), dma((2,)), dma((3,)), dma((3,)),
                 dma((CHUNKS,)), dma((CHUNKS,)), dma((CHUNKS,)), dma((CHUNKS,)), dma((CHUNKS,)), dma((CHUNKS,)), dma((CHUNKS,)),
                 dma((UNITS,)), dma((UNITS,)), dma((UNITS,)), dma((UNITS,)), dma((UNITS,)), dma((UNITS,)), dma((4, UNITS)),
-                dma((2,)), dma((2,)), dma((PIECES, 3)), dma((PIECES,)), dma((PIECES,)), dma((PIECES,)), dma((PIECES,)),
+                dma((2, 2)), dma((2,)), dma((PIECES, 3)), dma((PIECES,)), dma((PIECES,)), dma((PIECES,)), dma((PIECES,)), dma((PIECES,)), dma((2,)),
             ],
             compiler_params=pltpu.CompilerParams(collective_id=0, has_side_effects=True, vmem_limit_bytes=67043328),
             name='moe_ring',
-        )(tokens, expert_idx, gates, w_gate, w_up, w_down)
+        )(tokens, expert_idx.T, gates.T, w_gate, w_up, w_down)
         return out
 
     return jax.shard_map(device_step, mesh=mesh, in_specs=(row_spec, row_spec, row_spec, P('ep', 'fsdp', None), P('ep', 'fsdp', None), P('ep', None, 'fsdp')), out_specs=row_spec, check_vma=False)

time: 265 us -> 252 us (0.951)
  Pallas kernels: 259 us -> 247 us
  local copies, waits for them, and re-layouts: 5.79 us -> 2.65 us
    pallas_call x1, Pallas kernels: 259 us -> 247 us  [device_step(): pl.pallas_call(functools.partial(moe_kernel, cap), out_shape=(jax.ShapeDt...]
    unnamed x3 -> x1, local copies, waits for them, and re-layouts: 5.79 us -> 2.65 us
where the time goes in v2:
time: 252 us; the launch traced here: 250 us
  Pallas kernels  247 us (98%)
  local copies, waits for them, and re-layouts  2.65 us (1%)
    pallas_call x1, Pallas kernels, device_step(): pl.pallas_call(functools.partial(moe_kernel, cap), out_shape=(jax.ShapeDt...  247 us

profile of v2, /device:TPU:97, one launch (start us, length us, event | category | flops | bytes accessed | tf_op | source)
XLA Modules:
  0.0 250.0 jit_solution(1917092153493367386)
XLA Ops:
  0.0 247.3 %moe_ring.1 = (bf16[512,1536]{1,0:T(8,128)(2,1)}, bf16[10,2,4,2,384,256]{5,4,3,2,1,0:T(8,128)(2,1)}, bf16[12,10,512,128]{3,2,1,0:T(8,128)(2,1)}) custom-call(bf16[512,1536]{1,0:T(8,128)(2,1)} %tok_in.1, s32[8,512]{1,0:T(8,128)} %bitcast.2, f32[8,512]{1,0:T(8,128)} %bitcast.3, bf16[5,384,512]{2,1,0:T(8,128)(2,1)} %wg.1, bf16[5,384,512]{2,1,0:T(8,128)(2,1)} %wu.1, ...), custom_call_target="tpu_custom_call" | custom-call | tf_op jit(solution)/shard_map/moe_ring/pallas_call | solution.py:514
  247.3 2.7 %copy.8 = bf16[512,1536]{1,0:T(8,128)(2,1)} copy(bf16[512,1536]{1,0:T(8,128)(2,1)} %get-tuple-element.6) | data formatting | bytes 3145728

commit v3 on v2

--- a/solution.py
+++ b/solution.py
@@ -14,15 +14,16 @@
 RING = 4
 CHUNKS = 10
 UNITS = 3
+EARLY = 1
 PIECES = 6
 
 
 def moe_kernel(cap, tok_in, idx_ref, gates_ref, wg, wu, wd, out_ref, gu_land, d_land,
-               tok, wbuf, hid, wdb, wlast, accs, in_a, in_b, in_l, in_r, gsrc, grecv, gcol, stage,
+               tok, wbuf, hid, wdb, mlast, wlast, accs, in_a, in_b, in_l, in_r, gsrc, grecv, gcol, stage,
                tload, tsend, trecv, tfar, gsend, grsem,
                ysend, ssend, from_l, from_r, far_a, far_b, from_s,
                dysend, dssend, dfrom_l, dfrom_r, dfar_a, dfar_b, dfrom_s,
-               lsem, dlsem, asend, asem, bsem, lsum, rsum, osem, efwd):
+               lsem, dlsem, asend, asem, bsem, lsum, rsum, osem, efwd, mload):
     rows = tok_in.shape[0]
     half = rows // 2
     n_local, shard, ffn = wg.shape
@@ -81,39 +82,60 @@
         send(fref, fref, ssend.at[n], from_s.at[n], sib)
 
     last = CHUNKS - 1
-    le, lf = last // 2, last % 2
+    le = last // 2
     top, low = slice(0, hs), slice(hs, shard)
 
-    def to_sib_last(shard_id, ref):
-        for m in range(2):
-            send(ref(m), wlast.at[shard_id, :, m * fh:(m + 1) * fh], ssend.at[last], from_s.at[last], sib)
-
-    def own_last():
-        for dev, order, early, late in ((y_r, (top, low), 0, from_l), (y_l, (low, top), 1, from_r)):
-            for part, rsem in zip(order, (efwd.at[early], late.at[last])):
-                for m, w in enumerate((wg, wu)):
-                    send(w.at[le, part, lf * fh:(lf + 1) * fh], gu_land.at[mine + le, lf, q, m, part],
-                         ysend.at[last], rsem, dev)
-        to_sib_last(q, lambda m: (wg, wu)[m].at[le, :, lf * fh:(lf + 1) * fh])
-
-    def fwd_last():
-        la = gu_land.at[mine + le, lf, q_l, :, top]
-        wait(la, efwd.at[0])
-        send(la, la, ysend.at[last], far_a.at[last], y_r)
-        rb = gu_land.at[mine + le, lf, q_r, :, low]
-        wait(rb, efwd.at[1])
-        send(rb, rb, ysend.at[last], far_b.at[last], y_l)
-
-    def near_last():
-        wait(gu_land.at[mine + le, lf, q_l, :, low], from_l.at[last])
-        to_sib_last(q_l, lambda m: gu_land.at[mine + le, lf, q_l, m])
-        wait(gu_land.at[mine + le, lf, q_r, :, top], from_r.at[last])
-        to_sib_last(q_r, lambda m: gu_land.at[mine + le, lf, q_r, m])
-
-    def far_last():
-        wait(gu_land.at[mine + le, lf, q_f, :, top], far_a.at[last])
-        wait(gu_land.at[mine + le, lf, q_f, :, low], far_b.at[last])
-        to_sib_last(q_f, lambda m: gu_land.at[mine + le, lf, q_f, m])
+    def piece_of(n, shard_id, part):
+        e, f = n // 2, n % 2
+        if n == last:
+            return mlast.at[shard_id, part]
+        return gu_land.at[mine + e, f, shard_id, :, part]
+
+    def to_sib(n, shard_id):
+        e, f = n // 2, n % 2
+        src = piece_of(n, shard_id, slice(0, shard))
+        dst = wlast.at[shard_id] if n == last else src
+        send(src, dst, ssend.at[n], from_s.at[n], sib)
+
+    def own_half(n):
+        e, f = n // 2, n % 2
+
+        def put(dev, part, sem, rsem):
+            for m, w in enumerate((wg, wu)):
+                if n == last:
+                    dst = mlast.at[q, part, m * fh:(m + 1) * fh]
+                else:
+                    dst = gu_land.at[mine + e, f, q, m, part]
+                send(w.at[e, part, f * fh:(f + 1) * fh], dst, sem, rsem, dev)
+
+        put(y_r, top, ysend.at[n], efwd.at[last - n, 0])
+        put(y_l, low, ysend.at[n], efwd.at[last - n, 1])
+        put(y_r, low, ysend.at[n], from_l.at[n])
+        put(y_l, top, ysend.at[n], from_r.at[n])
+        if n == last:
+            wait(mlast.at[q], mload)
+            to_sib(n, q)
+        else:
+            put(sib, slice(0, shard), ssend.at[n], from_s.at[n])
+
+    def fwd_half(n):
+        la = piece_of(n, q_l, top)
+        wait(la, efwd.at[last - n, 0])
+        send(la, la, ysend.at[n], far_a.at[n], y_r)
+        rb = piece_of(n, q_r, low)
+        wait(rb, efwd.at[last - n, 1])
+        send(rb, rb, ysend.at[n], far_b.at[n], y_l)
+
+    def near_half(n):
+        wait(piece_of(n, q_l, low), from_l.at[n])
+        to_sib(n, q_l)
+        wait(piece_of(n, q_r, top), from_r.at[n])
+        to_sib(n, q_r)
+
+    def far_half(n):
+        wait(piece_of(n, q_f, top), far_a.at[n])
+        wait(piece_of(n, q_f, low), far_b.at[n])
+        to_sib(n, q_f)
 
     def own_d():
         for dev, ssem, rsem in ((y_r, dysend, dfrom_l), (y_l, dysend, dfrom_r)):
@@ -192,13 +214,16 @@
         pl.semaphore_signal(barrier, inc=1, device_id=dev, device_id_type=MESH)
     pl.semaphore_wait(barrier, 6)
 
+    own_gu(0)
+    own_gu(1)
     own_tok = pltpu.make_async_copy(tok_in, tok.at[0], tload)
     own_tok.start()
     send(tok_in, tok.at[1], tsend.at[0], trecv.at[0], x_r)
     send(tok_in, tok.at[2], tsend.at[1], trecv.at[1], x_l)
-    own_gu(0)
-    own_gu(1)
     own_d_sib()
+    for m, w in enumerate((wg, wu)):
+        pltpu.make_async_copy(w.at[le, :, fh * (last % 2):fh * (last % 2 + 1)],
+                              mlast.at[q, :, m * fh:(m + 1) * fh], mload).start()
 
     expert = lax.broadcasted_iota(jnp.int32, (128, rows), 0)
     chosen = jnp.zeros((128, rows), F32)
@@ -299,43 +324,50 @@
 
     def steady(n, carry):
         loaded(n, 0)
-        gu_items(n, 0, 0, 4)
-
-        @pl.when(n == CHUNKS - 2)
-        def _():
-            near_last()
+        gu_items(n, 0, 0, 2)
+
+        @pl.when(n == last - 1)
+        def _():
+            fwd_half(last)
             own_d()
+
+        gu_items(n, 0, 2, 4)
+
+        @pl.when(n == last - 2)
+        def _():
+            near_half(last - 1)
             load_piece(0)
 
         loaded(n, 1)
         gu_items(n, 1, 0, 2)
 
-        @pl.when(n <= CHUNKS - 4)
+        @pl.when(n <= last - 4)
         def _():
             fwd_gu(n + 2)
 
-            @pl.when(n <= 4)
-            def _():
-                own_gu(n + 4)
-
-            @pl.when(n == CHUNKS - 4)
-            def _():
-                own_last()
-
-        @pl.when(n <= CHUNKS - 3)
+            @pl.when(n == 3)
+            def _():
+                own_gu(7)
+
+            @pl.when(n == last - 4)
+            def _():
+                own_half(last - 1)
+
+        @pl.when(n <= last - 2)
         def _():
             far_gu(n + 1)
             load_mine(n + 1)
 
         gu_items(n, 1, 2, 4)
 
-        @pl.when(n <= CHUNKS - 3)
+        @pl.when(n <= last - 2)
         def _():
             load_theirs(n + 1)
 
-        @pl.when(n == CHUNKS - 3)
-        def _():
-            fwd_last()
+        @pl.when(n == last - 3)
+        def _():
+            fwd_half(last - 1)
+            own_half(last)
 
         @pl.when(n == 5)
         def _():
@@ -347,8 +379,7 @@
         return carry
 
     lax.fori_loop(3, CHUNKS - 1, steady, 0)
-    far_last()
-    load_mine(last)
+    near_half(last)
 
     def finish(p):
         s = p % 2
@@ -384,8 +415,15 @@
             total = o if total is None else total + o
         return total
 
+    def first_part(i, carry):
+        @pl.when(i == EARLY)
+        def _():
+            far_half(last)
+        accs[0, i] = combine(0, 3 - i, early_experts)
+        return carry
+
     wait(wdb.at[0], dlsem.at[0])
-    accs[0, 0] = combine(0, 3, early_experts)
+    lax.fori_loop(0, EARLY + 1, first_part, 0)
 
     def block_step(t, carry):
         p, i = t // 4, t % 4
@@ -402,19 +440,20 @@
 
         @pl.when(p == 0)
         def _():
-            @pl.when(i > 0)
+            @pl.when(i > EARLY)
             def _():
                 accs[0, i] = combine(0, b, early_experts)
 
-            @pl.when(i == 0)
-            def _():
-                loaded(last, 0)
-            gu_item(last, 0, b)
+            gu_item(last, 0, b, mlast)
 
             @pl.when(i == 0)
             def _():
                 wait(wlast, from_s.at[last])
             gu_item(last, 1, b, wlast)
+
+            @pl.when(i == 3)
+            def _():
+                fwd_d(0)
             accs[0, i] += combine(0, b, last_experts)
 
         @pl.when(p > 0)
@@ -425,14 +464,6 @@
         def _():
             send(accs.at[s, 0, 0:half], in_a.at[p], asend.at[p, 0], asem.at[p], x_r)
             send(accs.at[s, 0, half:rows], in_b.at[p], asend.at[p, 0], bsem.at[p], x_l)
-
-            @pl.when(p == 1)
-            def _():
-                fwd_d(1)
-
-            @pl.when(p == 2)
-            def _():
-                fwd_d(2)
 
             @pl.when(p == 3)
             def _():
@@ -457,18 +488,21 @@
             accs[s, 2, half:rows] += in_b[p]
             send(accs.at[s, 2, half:rows], in_r.at[p, half:rows], asend.at[p, 2], rsum.at[p], x_l)
 
-            @pl.when(p == 0)
-            def _():
-                fwd_d(0)
-
+            for k in (1, 2):
+                @pl.when(p == k)
+                def _(k=k):
+                    fwd_d(k)
+
+        @pl.when(i == 3)
+        def _():
             for k in range(1, PIECES):
                 @pl.when(p == k - 1)
                 def _(k=k):
                     load_piece(k)
 
-        @pl.when((i == 3) & (p >= 1))
-        def _():
-            finish(p - 1)
+            @pl.when(p >= 1)
+            def _():
+                finish(p - 1)
         return carry
 
     lax.fori_loop(0, 4 * PIECES, block_step, 0)
@@ -526,6 +560,7 @@
                 pltpu.VMEM((2 * n_local, 4, rows, ffn), BF16),
                 pltpu.VMEM((2, 2 * n_local, ffn, piece), BF16),
                 pltpu.VMEM((RING, shard, ffn), BF16),
+                pltpu.VMEM((RING, shard, ffn), BF16),
                 pltpu.VMEM((2, 4, rows, piece), F32),
                 pltpu.VMEM((PIECES, half, piece), F32),
                 pltpu.VMEM((PIECES, half, piece), F32),
@@ -538,7 +573,7 @@
                 dma, dma((4,)), dma((2,)), dma((2,)), dma((3,)), dma((3,)),
                 dma((CHUNKS,)), dma((CHUNKS,)), dma((CHUNKS,)), dma((CHUNKS,)), dma((CHUNKS,)), dma((CHUNKS,)), dma((CHUNKS,)),
                 dma((UNITS,)), dma((UNITS,)), dma((UNITS,)), dma((UNITS,)), dma((UNITS,)), dma((UNITS,)), dma((4, UNITS)),
-                dma((2, 2)), dma((2,)), dma((PIECES, 3)), dma((PIECES,)), dma((PIECES,)), dma((PIECES,)), dma((PIECES,)), dma((PIECES,)), dma((2,)),
+                dma((2, 2)), dma((2,)), dma((PIECES, 3)), dma((PIECES,)), dma((PIECES,)), dma((PIECES,)), dma((PIECES,)), dma((PIECES,)), dma((2, 2)), dma,
             ],
             compiler_params=pltpu.CompilerParams(collective_id=0, has_side_effects=True, vmem_limit_bytes=67043328),
             name='moe_ring',

time: 252 us -> 251 us (level)
  no operation moved by 1% of the time
where the time goes in v3:
time: 251 us; the launch traced here: 250 us
  Pallas kernels  247 us (98%)
  local copies, waits for them, and re-layouts  2.65 us (1%)
    pallas_call x1, Pallas kernels, device_step(): pl.pallas_call(functools.partial(moe_kernel, cap), out_shape=(jax.ShapeDt...  247 us

profile of v3, /device:TPU:97, one launch (start us, length us, event | category | flops | bytes accessed | tf_op | source)
XLA Modules:
  0.0 250.2 jit_solution(10241548754187473590)
XLA Ops:
  0.0 247.5 %moe_ring.1 = (bf16[512,1536]{1,0:T(8,128)(2,1)}, bf16[10,2,4,2,384,256]{5,4,3,2,1,0:T(8,128)(2,1)}, bf16[12,10,512,128]{3,2,1,0:T(8,128)(2,1)}) custom-call(bf16[512,1536]{1,0:T(8,128)(2,1)} %tok_in.1, s32[8,512]{1,0:T(8,128)} %bitcast.2, f32[8,512]{1,0:T(8,128)} %bitcast.3, bf16[5,384,512]{2,1,0:T(8,128)(2,1)} %wg.1, bf16[5,384,512]{2,1,0:T(8,128)(2,1)} %wu.1, ...), custom_call_target="tpu_custom_call" | custom-call | tf_op jit(solution)/shard_map/moe_ring/pallas_call | solution.py:548
  247.5 2.7 %copy.8 = bf16[512,1536]{1,0:T(8,128)(2,1)} copy(bf16[512,1536]{1,0:T(8,128)(2,1)} %get-tuple-element.6) | data formatting | bytes 3145728

commit v4 on v3

--- a/solution.py
+++ b/solution.py
@@ -358,16 +358,16 @@
             far_gu(n + 1)
             load_mine(n + 1)
 
-        gu_items(n, 1, 2, 4)
-
-        @pl.when(n <= last - 2)
-        def _():
-            load_theirs(n + 1)
-
         @pl.when(n == last - 3)
         def _():
             fwd_half(last - 1)
             own_half(last)
+
+        gu_items(n, 1, 2, 4)
+
+        @pl.when(n <= last - 2)
+        def _():
+            load_theirs(n + 1)
 
         @pl.when(n == 5)
         def _():

time: 251 us -> 250 us (level)
  no operation moved by 1% of the time
where the time goes in v4:
time: 250 us; the launch traced here: 249 us
  Pallas kernels  247 us (99%)
  local copies, waits for them, and re-layouts  2.65 us (1%)
    pallas_call x1, Pallas kernels, device_step(): pl.pallas_call(functools.partial(moe_kernel, cap), out_shape=(jax.ShapeDt...  247 us

profile of v4, /device:TPU:97, one launch (start us, length us, event | category | flops | bytes accessed | tf_op | source)
XLA Modules:
  0.0 249.5 jit_solution(15627347307636672770)
XLA Ops:
  0.0 246.8 %moe_ring.1 = (bf16[512,1536]{1,0:T(8,128)(2,1)}, bf16[10,2,4,2,384,256]{5,4,3,2,1,0:T(8,128)(2,1)}, bf16[12,10,512,128]{3,2,1,0:T(8,128)(2,1)}) custom-call(bf16[512,1536]{1,0:T(8,128)(2,1)} %tok_in.1, s32[8,512]{1,0:T(8,128)} %bitcast.2, f32[8,512]{1,0:T(8,128)} %bitcast.3, bf16[5,384,512]{2,1,0:T(8,128)(2,1)} %wg.1, bf16[5,384,512]{2,1,0:T(8,128)(2,1)} %wu.1, ...), custom_call_target="tpu_custom_call" | custom-call | tf_op jit(solution)/shard_map/moe_ring/pallas_call | solution.py:548
  246.8 2.7 %copy.8 = bf16[512,1536]{1,0:T(8,128)(2,1)} copy(bf16[512,1536]{1,0:T(8,128)(2,1)} %get-tuple-element.6) | data formatting | bytes 3145728
